TPU v7x, 32 devices: a whole 2x2x4 slice. The times are simulated.
32 devices in a mesh: study: 2 (over x), ky: 16 (over z, y, core).
Axes of the slice: x: 2, y: 2, z: 4, core: 2. Of those that a mesh axis runs over, the one named last changes fastest.
Arguments:
- kspace: bfloat16 [32, 2, 32, 256, 256], P('study', None, None, 'ky'), parts along dimension 0, may hold values from -6 to 6
- kernel: bfloat16 [2, 768, 64], replicated, may hold values from -0.21875 to 0.21875
- pattern: int32 [32], P('study'), parts along dimension 0, may hold values from 0 to 2
- offsets: int32 [4], replicated, may hold values from -2 to 2
- segment: int32 [256], replicated, may hold values from 0 to 2
- temporal_basis: float32 [5, 16], replicated, may hold values from -1.5 to 1.5
Outputs:
- basis_images: float32 [10, 2, 32, 256, 256], P('study', None, None, 'ky'), parts along dimension 0
There are 2 independent parts, one for each index of `study`. A program takes and returns all parts, laid end to end along the dimension named above; an argument that names none is the same for every part. Nothing has to cross between parts.
All inputs are finite; a program needn't handle non-finite values.
Results may differ from a plain program's by a relative error of at most 0.0003.
Values may be sent and summed in bfloat16 or wider, within the bound.
No kernel may reach another device: no remote copies, remote signals or barrier semaphores. Data moves between devices by JAX's collectives and lax.ppermute only.
A program may use at most 192 MiB of HBM per device.

v0:
```python
import jax
import jax.numpy as jnp
from jax import lax
from jax.sharding import PartitionSpec as P

frame_block = 4


def padded_2(block, sides, width):
    for axis, dim in sides:
        count = lax.axis_size(axis)
        forward = [(i, i + 1) for i in range(count - 1)]
        backward = [(target, source) for source, target in forward]
        low = lax.ppermute(
            lax.slice_in_dim(block, block.shape[dim] - width, None, axis=dim), axis, forward
        )
        high = lax.ppermute(lax.slice_in_dim(block, 0, width, axis=dim), axis, backward)
        block = jnp.concatenate([low, block, high], axis=dim)
    return block


def inverse_rows(spectra):
    row_total = spectra.shape[3]
    row_index = jnp.arange(row_total, dtype=jnp.int32)
    phase_index = row_index[:, None] * row_index[None, :] % row_total
    phase_angle = phase_index.astype(jnp.float32) * (2.0 * jnp.pi / row_total)
    cosine_table = jnp.cos(phase_angle)
    sine_table = jnp.sin(phase_angle)
    real_part = spectra[:, 0]
    imag_part = spectra[:, 1]
    high = lax.Precision.HIGHEST
    out_real = jnp.einsum("yk,mckx->mcxy", cosine_table, real_part, precision=high) - jnp.einsum(
        "yk,mckx->mcxy", sine_table, imag_part, precision=high
    )
    out_imag = jnp.einsum("yk,mckx->mcxy", sine_table, real_part, precision=high) + jnp.einsum(
        "yk,mckx->mcxy", cosine_table, imag_part, precision=high
    )
    scale = 1.0 / jnp.sqrt(jnp.float32(row_total))
    return jnp.stack([out_real, out_imag], axis=1) * scale


def on_device(kspace, kernel, pattern, offsets, segment, temporal_basis):
    frame_total, _, coil_count, row_count, kx_count = kspace.shape
    group_count = kernel.shape[0]
    group_frames = frame_total // group_count
    row_start = lax.axis_index("ky") * row_count
    local_segment = lax.dynamic_slice_in_dim(segment, row_start, row_count)
    acquired = (local_segment[None, :] == pattern[:, None])[:, None, None, :, None]
    zero_fill = jnp.where(acquired, kspace, jnp.zeros_like(kspace))
    padded = padded_2(zero_fill, (("ky", 3),), 1)
    blocks = frame_total // frame_block
    padded_blocks = padded.reshape(blocks, frame_block, 2, coil_count, row_count + 2, kx_count)
    block_group = jnp.arange(blocks, dtype=jnp.int32) * frame_block // group_frames

    def estimate_block(block_item):
        block_data, group_index = block_item
        ky_layers = []
        for ky_tap in range(3):
            ky_slice = block_data[:, :, :, ky_tap : ky_tap + row_count, :]
            ky_layers.append(
                jnp.stack(
                    [
                        jnp.roll(ky_slice, -offsets[kx_tap], axis=4)
                        for kx_tap in range(offsets.shape[0])
                    ],
                    axis=2,
                )
            )
        sources = jnp.stack(ky_layers, axis=2).reshape(frame_block, -1, row_count * kx_count)
        weights = lax.dynamic_index_in_dim(kernel, group_index, 0, keepdims=False)
        return jnp.einsum("io,fir->for", weights, sources, preferred_element_type=jnp.float32)

    estimate = lax.map(estimate_block, (padded_blocks, block_group))
    estimate = estimate.reshape(frame_total, 2, coil_count, row_count, kx_count)
    filled = jnp.where(acquired, kspace.astype(jnp.float32), estimate)
    high = lax.Precision.HIGHEST
    coefficients = jnp.einsum("bf,fpcrx->bpcrx", temporal_basis, filled, precision=high)
    swapped = lax.all_to_all(coefficients, "ky", split_axis=4, concat_axis=3, tiled=True)
    return inverse_rows(swapped)


def solution(mesh):
    return jax.shard_map(
        on_device,
        mesh=mesh,
        in_specs=(P("study", None, None, "ky", None), P(), P("study"), P(), P(), P()),
        out_specs=P("study", None, None, "ky", None),
        check_vma=False,
    )
```

profile of v0, /device:TPU:1, one launch (start us, length us, event | category | flops | bytes accessed | tf_op | source)
XLA Modules:
  0.0 754.4 jit_solution(11994539295915836448)
XLA Ops:
  31.8 13.5 %pad_maximum_fusion.1 = bf16[16,2,32,18,256]{4,3,2,1,0:T(8,128)(2,1)} fusion(bf16[16,2,32,1,256]{4,3,2,1,0:T(2,128)(2,1)S(1)} %copy.40, bf16[16,2,32,16,256]{4,3,2,1,0:T(8,128)(2,1)} %broadcast_select_fusion, bf16[16,2,32,1,256]{4,3,2,1,0:T(2,128)(2,1)S(1)} %copy.39), kind=kLoop, calls=%fused_computation.61 | loop fusion | flops 28311552 | bytes 18874368 | tf_op jit(solution)/shard_map/concatenate | solution.py:18
  45.4 419.9 %while.12 = (s32[]{:T(128)}, f32[4,4,64,4096]{3,2,1,0:T(8,128)}, bf16[4,4,2,32,18,256]{5,4,3,2,1,0:T(8,128)(2,1)}, s32[]{:T(128)}, s32[]{:T(128)}, /*index=5*/s3...) while((s32[]{:T(128)}, f32[4,4,64,4096]{3,2,1,0:T(8,128)}, ...), condition=%wide.region_1.3_spmd, body=%wide.region_0.2_spmd.sunk | while | flops 1723858944 | bytes 229213552 | solution.py:73
  72.6 11.5 %fusion.93 = (bf16[4,2,1,32,16,256]{5,4,3,2,1,0:T(8,128)(2,1)S(1)}, bf16[4,2,1,32,16,256]{5,4,3,2,1,0:T(8,128)(2,1)S(1)}, bf16[4,2,1,32,16,256]{5,4,3,2,1,0:T(8,128)(2,1)S(1)}, bf16[4,2,1,32,16,256]{5,4,3,2,1,0:T(8,128)(2,1)S(1)}) fusion(s32[]{:T(128)S(6)} %select_n.129, bf16[4,2,32,16,256]{4,3,2,1,0:T(8,128)(2,1)} %get-tuple-element.218, ...), kind=kLoop, calls=%fused_computation.34.clone.1 | loop fusion | flops 16777216 | bytes 10485776 | tf_op jit(solution)/shard_map/while/body/eval_jaxpr/stack | solution.py:61
  85.2 10.2 %pad_maximum_fusion.3 = bf16[4,2,3,4,32,16,256]{6,5,4,3,2,1,0:T(8,128)(2,1)} fusion(bf16[4,2,1,4,32,16,256]{6,5,4,3,2,1,0:T(8,128)(2,1)S(1)} %maximum_bitcast_fusion.5, bf16[4,2,1,4,32,16,256]{6,5,4,3,2,1,0:T(8,128)(2,1)S(1)} %get-tuple-element.233, bf16[4,2,1,4,32,16,256]{6,5,4,3,2,1,0:T(8,128)(2,1)S(1)} %get-tuple-element.234), kind=kLoop, calls=%fused_computation.clone.1 | loop fusion | flops 25165824 | bytes 50331648 | tf_op jit(solution)/shard_map/while/body/eval_jaxpr/stack | solution.py:69
  95.4 37.8 %reshape.50 = bf16[4,768,4096]{2,1,0:T(8,128)(2,1)} reshape(bf16[4,2,3,4,32,16,256]{6,5,4,3,2,1,0:T(8,128)(2,1)} %pad_maximum_fusion.3) | data formatting | bytes 50331648 | tf_op jit(solution)/shard_map/while/body/eval_jaxpr/reshape | solution.py:69
  135.8 14.8 %fusion.96 = f32[4,4,64,4096]{3,2,1,0:T(8,128)} fusion(f32[4,4,64,4096]{3,2,1,0:T(8,128)} %get-tuple-element.251, s32[]{:T(128)} %get-tuple-element.250, bf16[4,768,4096]{2,1,0:T(8,128)(2,1)} %reshape.50, bf16[2,768,64]{1,2,0:T(8,128)(2,1)S(1)} %get-tuple-element.273, s32[]{:T(128)S(6)} %select_n.136), kind=kOutput, calls=%fused_computation.29.clone.1 | convolution fusion | flops 1610612736 | bytes 29458948 | tf_op jit(solution)/shard_map/while/body/eval_jaxpr/io,fir->for/dot_general | solution.py:71
  177.5 11.5 %fusion.93 = (bf16[4,2,1,32,16,256]{5,4,3,2,1,0:T(8,128)(2,1)S(1)}, bf16[4,2,1,32,16,256]{5,4,3,2,1,0:T(8,128)(2,1)S(1)}, bf16[4,2,1,32,16,256]{5,4,3,2,1,0:T(8,128)(2,1)S(1)}, bf16[4,2,1,32,16,256]{5,4,3,2,1,0:T(8,128)(2,1)S(1)}) fusion(s32[]{:T(128)S(6)} %select_n.129, bf16[4,2,32,16,256]{4,3,2,1,0:T(8,128)(2,1)} %get-tuple-element.218, ...), kind=kLoop, calls=%fused_computation.34.clone.1 | loop fusion | flops 16777216 | bytes 10485776 | tf_op jit(solution)/shard_map/while/body/eval_jaxpr/stack | solution.py:61
  190.1 10.2 %pad_maximum_fusion.3 = bf16[4,2,3,4,32,16,256]{6,5,4,3,2,1,0:T(8,128)(2,1)} fusion(bf16[4,2,1,4,32,16,256]{6,5,4,3,2,1,0:T(8,128)(2,1)S(1)} %maximum_bitcast_fusion.5, bf16[4,2,1,4,32,16,256]{6,5,4,3,2,1,0:T(8,128)(2,1)S(1)} %get-tuple-element.233, bf16[4,2,1,4,32,16,256]{6,5,4,3,2,1,0:T(8,128)(2,1)S(1)} %get-tuple-element.234), kind=kLoop, calls=%fused_computation.clone.1 | loop fusion | flops 25165824 | bytes 50331648 | tf_op jit(solution)/shard_map/while/body/eval_jaxpr/stack | solution.py:69
  200.3 37.8 %reshape.50 = bf16[4,768,4096]{2,1,0:T(8,128)(2,1)} reshape(bf16[4,2,3,4,32,16,256]{6,5,4,3,2,1,0:T(8,128)(2,1)} %pad_maximum_fusion.3) | data formatting | bytes 50331648 | tf_op jit(solution)/shard_map/while/body/eval_jaxpr/reshape | solution.py:69
  240.7 14.7 %fusion.96 = f32[4,4,64,4096]{3,2,1,0:T(8,128)} fusion(f32[4,4,64,4096]{3,2,1,0:T(8,128)} %get-tuple-element.251, s32[]{:T(128)} %get-tuple-element.250, bf16[4,768,4096]{2,1,0:T(8,128)(2,1)} %reshape.50, bf16[2,768,64]{1,2,0:T(8,128)(2,1)S(1)} %get-tuple-element.273, s32[]{:T(128)S(6)} %select_n.136), kind=kOutput, calls=%fused_computation.29.clone.1 | convolution fusion | flops 1610612736 | bytes 29458948 | tf_op jit(solution)/shard_map/while/body/eval_jaxpr/io,fir->for/dot_general | solution.py:71
  282.3 11.5 %fusion.93 = (bf16[4,2,1,32,16,256]{5,4,3,2,1,0:T(8,128)(2,1)S(1)}, bf16[4,2,1,32,16,256]{5,4,3,2,1,0:T(8,128)(2,1)S(1)}, bf16[4,2,1,32,16,256]{5,4,3,2,1,0:T(8,128)(2,1)S(1)}, bf16[4,2,1,32,16,256]{5,4,3,2,1,0:T(8,128)(2,1)S(1)}) fusion(s32[]{:T(128)S(6)} %select_n.129, bf16[4,2,32,16,256]{4,3,2,1,0:T(8,128)(2,1)} %get-tuple-element.218, ...), kind=kLoop, calls=%fused_computation.34.clone.1 | loop fusion | flops 16777216 | bytes 10485776 | tf_op jit(solution)/shard_map/while/body/eval_jaxpr/stack | solution.py:61
  305.1 37.8 %reshape.50 = bf16[4,768,4096]{2,1,0:T(8,128)(2,1)} reshape(bf16[4,2,3,4,32,16,256]{6,5,4,3,2,1,0:T(8,128)(2,1)} %pad_maximum_fusion.3) | data formatting | bytes 50331648 | tf_op jit(solution)/shard_map/while/body/eval_jaxpr/reshape | solution.py:69
  345.5 14.7 %fusion.96 = f32[4,4,64,4096]{3,2,1,0:T(8,128)} fusion(f32[4,4,64,4096]{3,2,1,0:T(8,128)} %get-tuple-element.251, s32[]{:T(128)} %get-tuple-element.250, bf16[4,768,4096]{2,1,0:T(8,128)(2,1)} %reshape.50, bf16[2,768,64]{1,2,0:T(8,128)(2,1)S(1)} %get-tuple-element.273, s32[]{:T(128)S(6)} %select_n.136), kind=kOutput, calls=%fused_computation.29.clone.1 | convolution fusion | flops 1610612736 | bytes 29458948 | tf_op jit(solution)/shard_map/while/body/eval_jaxpr/io,fir->for/dot_general | solution.py:71
  387.1 11.5 %fusion.93 = (bf16[4,2,1,32,16,256]{5,4,3,2,1,0:T(8,128)(2,1)S(1)}, bf16[4,2,1,32,16,256]{5,4,3,2,1,0:T(8,128)(2,1)S(1)}, bf16[4,2,1,32,16,256]{5,4,3,2,1,0:T(8,128)(2,1)S(1)}, bf16[4,2,1,32,16,256]{5,4,3,2,1,0:T(8,128)(2,1)S(1)}) fusion(s32[]{:T(128)S(6)} %select_n.129, bf16[4,2,32,16,256]{4,3,2,1,0:T(8,128)(2,1)} %get-tuple-element.218, ...), kind=kLoop, calls=%fused_computation.34.clone.1 | loop fusion | flops 16777216 | bytes 10485776 | tf_op jit(solution)/shard_map/while/body/eval_jaxpr/stack | solution.py:61
  409.9 37.8 %reshape.50 = bf16[4,768,4096]{2,1,0:T(8,128)(2,1)} reshape(bf16[4,2,3,4,32,16,256]{6,5,4,3,2,1,0:T(8,128)(2,1)} %pad_maximum_fusion.3) | data formatting | bytes 50331648 | tf_op jit(solution)/shard_map/while/body/eval_jaxpr/reshape | solution.py:69
  450.2 14.7 %fusion.96 = f32[4,4,64,4096]{3,2,1,0:T(8,128)} fusion(f32[4,4,64,4096]{3,2,1,0:T(8,128)} %get-tuple-element.251, s32[]{:T(128)} %get-tuple-element.250, bf16[4,768,4096]{2,1,0:T(8,128)(2,1)} %reshape.50, bf16[2,768,64]{1,2,0:T(8,128)(2,1)S(1)} %get-tuple-element.273, s32[]{:T(128)S(6)} %select_n.136), kind=kOutput, calls=%fused_computation.29.clone.1 | convolution fusion | flops 1610612736 | bytes 29458948 | tf_op jit(solution)/shard_map/while/body/eval_jaxpr/io,fir->for/dot_general | solution.py:71
  465.3 11.0 %copy.54 = f32[128,8,16,256]{3,2,1,0:T(8,128)S(1)} copy(f32[128,8,16,256]{3,1,2,0:T(8,128)} %bitcast.126) | data formatting | bytes 33554432
  482.5 17.8 %fusion.30 = f32[5,2,32,16,256]{4,0,3,2,1:T(8,128)} fusion(f32[16,2,32,16,256]{4,3,2,1,0:T(8,128)S(1)} %convert_select_fusion, f32[5,16]{1,0:T(8,128)S(1)} %copy-done), kind=kOutput, calls=%fused_computation.64 | convolution fusion | flops 251658240 | bytes 22020416 | tf_op jit(solution)/shard_map/bf,fpcrx->bpcrx/dot_general | solution.py:77
  500.3 14.0 %copy.42 = f32[5,2,32,16,256]{2,3,1,0,4:T(8,128)} copy(f32[5,2,32,16,256]{4,0,3,2,1:T(8,128)} %fusion.30) | data formatting | bytes 10485760 | tf_op jit(solution)/shard_map/bf,fpcrx->bpcrx/dot_general | solution.py:77
  514.2 18.0 %reshape.47 = f32[16,1,81920]{2,1,0:T(1,128)} reshape(f32[256,5,2,16,32]{4,3,2,1,0:T(8,128)} %bitcast.122) | data formatting | bytes 10485760
  532.2 121.4 %all_to_all.18 = f32[16,1,81920]{2,1,0:T(1,128)} all-to-all(f32[16,1,81920]{2,1,0:T(1,128)} %reshape.47), channel_id=1, replica_groups=mesh['study'=2,'ky'=16] {'ky'}, dimensions={0} | all-to-all | bytes 10485760 | tf_op jit(solution)/shard_map/all_to_all | solution.py:78
  654.2 16.9 %reduce = f32[16,81920]{1,0:T(8,128)} reduce(f32[16,1,81920]{2,1,0:T(1,128)} %all_to_all.18, f32[]{:T(128)} %broadcast.61), dimensions={1}, to_apply=%all_to_all.13.reduce_sub_computation | reduce | bytes 10485764 | tf_op jit(solution)/shard_map/all_to_all | solution.py:78
  671.1 18.1 %reshape.48 = f32[256,5,2,16,32]{4,3,2,1,0:T(8,128)} reshape(f32[16,81920]{1,0:T(8,128)} %reduce) | data formatting | bytes 10485760
  689.2 18.5 %copy.44 = f32[5,2,32,16,16,16]{2,5,4,3,1,0:T(8,128)S(1)} copy(f32[5,2,32,16,16,16]{2,4,1,0,5,3:T(8,128)} %bitcast.123) | data formatting | bytes 10485760 | tf_op jit(solution)/shard_map/all_to_all | solution.py:78
  (68 shorter events, 217.1 us)
Async XLA Ops:
  0.0 482.5 %copy-start = (f32[5,16]{1,0:T(8,128)S(1)}, f32[5,16]{1,0:T(8,128)}, u32[]{:S(2)}) copy-start(f32[5,16]{1,0:T(8,128)} %param.15) | copy-start | bytes 964
  1.5 7.2 copy-start.3
  8.7 11.3 %copy-start.5 = (s32[4]{0:T(128)S(1)}, s32[4]{0:T(128)}, u32[]{:S(2)}) copy-start(s32[4]{0:T(128)} %param.13) | copy-start | bytes 52
  13.5 16.3 %collective-permute-start = (bf16[16,2,32,1,256]{4,2,3,1,0:T(8,128)(2,1)S(1)}, bf16[16,2,32,1,256]{4,2,3,1,0:T(8,128)(2,1)S(1)}, u32[]{:S(2)}, u32[]{:S(2)}) collective-permute-start(bf16[16,2,32,1,256]{4,2,3,1,0:T(8,128)(2,1)S(1)} %copy.37), channel_id=1, source_target_pairs={{0,1},{1,2},{2,3},{3,4},{4,5},{5,6},{6,7},{7,8},{8,9},{9,10},{10,1... | collective-permute-start | bytes 1572872 | tf_op jit(solution)/shard_map/ppermute | solution.py:14
  18.1 12.6 %collective-permute-start.1 = (bf16[16,2,32,1,256]{4,2,3,1,0:T(8,128)(2,1)S(1)}, bf16[16,2,32,1,256]{4,2,3,1,0:T(8,128)(2,1)S(1)}, u32[]{:S(2)}, u32[]{:S(2)}) collective-permute-start(bf16[16,2,32,1,256]{4,2,3,1,0:T(8,128)(2,1)S(1)} %copy.38), channel_id=1, source_target_pairs={{1,0},{2,1},{3,2},{4,3},{5,4},{6,5},{7,6},{8,7},{9,8},{10,9},{11,1... | collective-permute-start | bytes 1572872 | tf_op jit(solution)/shard_map/ppermute | solution.py:17
  31.8 13.6 %copy-start.2 = (bf16[2,768,64]{1,2,0:T(8,128)(2,1)S(1)}, bf16[2,768,64]{1,2,0:T(8,128)(2,1)}, u32[]{:S(2)}) copy-start(bf16[2,768,64]{1,2,0:T(8,128)(2,1)} %param.11) | copy-start | bytes 589828
  465.3 11.0 %copy-start.4 = (pred[16,16]{1,0:T(8,128)(4,1)S(1)}, pred[16,16]{1,0:T(8,128)(4,1)}, u32[]{:S(2)}) copy-start(pred[16,16]{1,0:T(8,128)(4,1)} %copy-done.3) | copy-start | bytes 772
  742.0 5.1 copy-start.1
where the time goes:
time: 765 us; the launch traced here: 754 us
  local copies, waits for them, and re-layouts  289 us (38%)
  other arithmetic  225 us (29%)
  blocking collectives  121 us (16%)
  matrix products  94.5 us (12%)
  loops' own time  8.59 us (1%)
    reshape x4, local copies, waits for them, and re-layouts, estimate_block(): jnp.stack(ky_layers, axis=2).reshape(frame_block, -1, row_count * kx_count)  151 us
    all_to_all x1, blocking collectives, on_device(): lax.all_to_all(coefficients, 'ky', split_axis=4, concat_axis=3, tiled=True)  121 us
    another operation x12, other arithmetic, estimate_block(): jnp.stack([jnp.roll(ky_slice, -offsets[kx_tap], axis=4) for kx_tap in ran...  111 us
    another operation x12, other arithmetic, estimate_block(): jnp.stack(ky_layers, axis=2).reshape(frame_block, -1, row_count * kx_count)  68.6 us
    unnamed x17, local copies, waits for them, and re-layouts  64.4 us
    dot_general x4, matrix products, estimate_block(): jnp.einsum('io,fir->for', weights, sources, preferred_element_type=jnp.fl...  58.8 us
    all_to_all x2, local copies, waits for them, and re-layouts, on_device(): lax.all_to_all(coefficients, 'ky', split_axis=4, concat_axis=3, tiled=True)  19 us
    dot_general x1, matrix products, on_device(): jnp.einsum('bf,fpcrx->bpcrx', temporal_basis, filled, precision=high)  17.8 us
  transfers between devices with their start and end apart: 2, of which 1 were waited for; matrix products, arithmetic and copies ran while one was open for 0% of the time, Pallas kernels for 0%

commit v1 on v0

--- a/solution.py
+++ b/solution.py
@@ -75,7 +75,19 @@
     filled = jnp.where(acquired, kspace.astype(jnp.float32), estimate)
     high = lax.Precision.HIGHEST
     coefficients = jnp.einsum("bf,fpcrx->bpcrx", temporal_basis, filled, precision=high)
-    swapped = lax.all_to_all(coefficients, "ky", split_axis=4, concat_axis=3, tiled=True)
+    ways, here = (lax.axis_size("ky"), lax.axis_index("ky"))
+    width_2 = coefficients.shape[4] // ways
+    shape = list(coefficients.shape)
+    shape[4] = width_2
+    height = shape[3]
+    shape[3] = height * ways
+    full = jnp.zeros(shape, coefficients.dtype)
+    for mask in range(ways):
+        part = lax.dynamic_slice_in_dim(coefficients, (here ^ mask) * width_2, width_2, axis=4)
+        if mask:
+            part = lax.ppermute(part, "ky", [(d, d ^ mask) for d in range(ways)])
+        full = lax.dynamic_update_slice_in_dim(full, part, (here ^ mask) * height, axis=3)
+    swapped = full
     return inverse_rows(swapped)
 
 

time: 765 us -> 1750 us (2.29)
  local copies, waits for them, and re-layouts: 289 us -> 1090 us
  waiting for transfers between devices: 6.45 us -> 290 us
  blocking collectives: 121 us -> 0 us
  starting transfers between devices: 6.45 us -> 29.3 us
    dynamic_update_slice x0 -> x16, local copies, waits for them, and re-layouts: none -> 770 us  [on_device(): lax.dynamic_update_slice_in_dim(full, part, (here ^ mask) * height, axis=3)]
    ppermute x0 -> x15, waiting for transfers between devices: none -> 284 us  [on_device(): part = lax.ppermute(part, 'ky', [(d, d ^ mask) for d in range(ways)])]
    all_to_all x1 -> x0, blocking collectives: 121 us -> none  [on_device(): lax.all_to_all(coefficients, 'ky', split_axis=4, concat_axis=3, tiled=True)]
    dynamic_slice x0 -> x17, local copies, waits for them, and re-layouts: none -> 83.6 us  [on_device(): lax.dynamic_slice_in_dim(coefficients, (here ^ mask) * width_2, width_2,...]
    unnamed x17 -> x21, local copies, waits for them, and re-layouts: 64.4 us -> 11.5 us
    ppermute x0 -> x15, local copies, waits for them, and re-layouts: none -> 37.3 us  [on_device(): part = lax.ppermute(part, 'ky', [(d, d ^ mask) for d in range(ways)])]
    ppermute x0 -> x15, starting transfers between devices: none -> 22.8 us  [on_device(): part = lax.ppermute(part, 'ky', [(d, d ^ mask) for d in range(ways)])]
    all_to_all x2 -> x0, local copies, waits for them, and re-layouts: 19 us -> none  [on_device(): lax.all_to_all(coefficients, 'ky', split_axis=4, concat_axis=3, tiled=True)]
  transfers between devices with their start and end apart: 2 -> 17, of which waited for: 1 -> 7; matrix products, arithmetic and copies ran while one was open for 0% -> 47% of each run, Pallas kernels for 0% -> 0%
where the time goes in v1:
time: 1750 us; the launch traced here: 1740 us
  local copies, waits for them, and re-layouts  1090 us (62%)
  waiting for transfers between devices  290 us (17%)
  other arithmetic  209 us (12%)
  matrix products  96.6 us (6%)
  starting transfers between devices  29.3 us (2%)
  loops' own time  20.4 us (1%)
    dynamic_update_slice x16, local copies, waits for them, and re-layouts, on_device(): lax.dynamic_update_slice_in_dim(full, part, (here ^ mask) * height, axis=3)  770 us
    ppermute x15, waiting for transfers between devices, on_device(): part = lax.ppermute(part, 'ky', [(d, d ^ mask) for d in range(ways)])  284 us
    reshape x4, local copies, waits for them, and re-layouts, estimate_block(): jnp.stack(ky_layers, axis=2).reshape(frame_block, -1, row_count * kx_count)  151 us
    another operation x12, other arithmetic, estimate_block(): jnp.stack([jnp.roll(ky_slice, -offsets[kx_tap], axis=4) for kx_tap in ran...  111 us
    dynamic_slice x17, local copies, waits for them, and re-layouts, on_device(): lax.dynamic_slice_in_dim(coefficients, (here ^ mask) * width_2, width_2,...  83.6 us
    another operation x12, other arithmetic, estimate_block(): jnp.stack(ky_layers, axis=2).reshape(frame_block, -1, row_count * kx_count)  68.8 us
    dot_general x4, matrix products, estimate_block(): jnp.einsum('io,fir->for', weights, sources, preferred_element_type=jnp.fl...  58.9 us
    ppermute x15, local copies, waits for them, and re-layouts, on_device(): part = lax.ppermute(part, 'ky', [(d, d ^ mask) for d in range(ways)])  37.3 us
  transfers between devices with their start and end apart: 17, of which 7 were waited for; matrix products, arithmetic and copies ran while one was open for 47% of the time, Pallas kernels for 0%

profile of v1, /device:TPU:1, one launch (start us, length us, event | category | flops | bytes accessed | tf_op | source)
XLA Modules:
  0.0 1739.1 jit_solution(924499190047031925)
XLA Ops:
  45.4 432.2 %while.12 = (s32[]{:T(128)}, f32[4,4,64,4096]{3,2,1,0:T(8,128)}, bf16[4,4,2,32,18,256]{5,4,3,2,1,0:T(8,128)(2,1)}, s32[]{:T(128)}, s32[]{:T(128)}, /*index=5*/s3...) while((s32[]{:T(128)}, f32[4,4,64,4096]{3,2,1,0:T(8,128)}, ...), condition=%wide.region_1.3_spmd, body=%wide.region_0.2_spmd.sunk | while | flops 1723858944 | bytes 229213552 | solution.py:73
  107.3 37.8 %reshape.48 = bf16[4,768,4096]{2,1,0:T(8,128)(2,1)} reshape(bf16[4,2,3,4,32,16,256]{6,5,4,3,2,1,0:T(8,128)(2,1)} %pad_maximum_fusion.3) | data formatting | bytes 50331648 | tf_op jit(solution)/shard_map/while/body/eval_jaxpr/reshape | solution.py:69
  212.3 37.8 %reshape.48 = bf16[4,768,4096]{2,1,0:T(8,128)(2,1)} reshape(bf16[4,2,3,4,32,16,256]{6,5,4,3,2,1,0:T(8,128)(2,1)} %pad_maximum_fusion.3) | data formatting | bytes 50331648 | tf_op jit(solution)/shard_map/while/body/eval_jaxpr/reshape | solution.py:69
  317.2 37.8 %reshape.48 = bf16[4,768,4096]{2,1,0:T(8,128)(2,1)} reshape(bf16[4,2,3,4,32,16,256]{6,5,4,3,2,1,0:T(8,128)(2,1)} %pad_maximum_fusion.3) | data formatting | bytes 50331648 | tf_op jit(solution)/shard_map/while/body/eval_jaxpr/reshape | solution.py:69
  422.1 37.8 %reshape.48 = bf16[4,768,4096]{2,1,0:T(8,128)(2,1)} reshape(bf16[4,2,3,4,32,16,256]{6,5,4,3,2,1,0:T(8,128)(2,1)} %pad_maximum_fusion.3) | data formatting | bytes 50331648 | tf_op jit(solution)/shard_map/while/body/eval_jaxpr/reshape | solution.py:69
  496.0 22.4 %fusion.28 = f32[2,32,16,256,5]{3,4,2,1,0:T(8,128)S(1)} fusion(f32[16,2,32,16,256]{4,3,2,1,0:T(8,128)} %convert_select_fusion, f32[5,16]{1,0:T(8,128)S(1)} %copy-done), kind=kOutput, calls=%fused_computation.58 | convolution fusion | flops 251658240 | bytes 22020416 | tf_op jit(solution)/shard_map/bf,fpcrx->bpcrx/dot_general | solution.py:77
  518.4 25.0 %dynamic-slice_bitcast_fusion.1 = (f32[5,2,32,16,16]{4,0,3,2,1:T(8,128)}, f32[5,2,32,16,16]{4,0,3,2,1:T(8,128)}, f32[5,2,32,16,16]{4,0,3,2,1:T(8,128)}, f32[5,2,...) fusion(f32[2,32,16,256,5]{3,4,2,1,0:T(8,128)S(1)} %fusion.28, ...), kind=kLoop, calls=%fused_computation.64 | loop fusion | bytes 10485824 | tf_op jit(solution)/shard_map/dynamic_slice | solution.py:86
  617.6 59.1 %collective-permute-done.6 = f32[5,2,32,16,16]{2,4,3,1,0:T(8,128)} collective-permute-done((f32[5,2,32,16,16]{2,4,3,1,0:T(8,128)}, f32[5,2,32,16,16]{2,4,3,1,0:T(8,128)}, u32[]{:S(2)}, u32[]{:S(2)}) %collective-permute-start.6) | collective-permute-done | bytes 327712 | tf_op jit(solution)/shard_map/ppermute | solution.py:88
  706.5 27.2 %collective-permute-done.8 = f32[5,2,32,16,16]{2,4,3,1,0:T(8,128)} collective-permute-done((f32[5,2,32,16,16]{2,4,3,1,0:T(8,128)}, f32[5,2,32,16,16]{2,4,3,1,0:T(8,128)}, u32[]{:S(2)}, u32[]{:S(2)}) %collective-permute-start.8) | collective-permute-done | bytes 327712 | tf_op jit(solution)/shard_map/ppermute | solution.py:88
  747.7 156.4 %collective-permute-done.11 = f32[5,2,32,16,16]{2,4,3,1,0:T(8,128)S(1)} collective-permute-done((f32[5,2,32,16,16]{2,4,3,1,0:T(8,128)}, f32[5,2,32,16,16]{2,4,3,1,0:T(8,128)S(1)}, u32[]{:S(2)}, u32[]{:S(2)}) %collective-permute-start.11) | collective-permute-done | bytes 327712 | tf_op jit(solution)/shard_map/ppermute | solution.py:88
  911.7 53.3 %dynamic_update_slice.54 = f32[5,2,32,256,16]{3,4,2,0,1:T(8,128)} dynamic-update-slice(f32[5,2,32,256,16]{3,4,2,0,1:T(8,128)} %broadcast_in_dim.34, f32[5,2,32,16,16]{3,4,2,0,1:T(8,128)S(1)} %copy.66, s32[]{:T(128)} %constant.91.clone.1, s32[]{:T(128)} %constant.91.clone.1, s32[]{:T(128)} %constant.91.clone.1, s32[]{:T(128)S(6)} %select_n.106, s32[]{:T(128)} %constant.91.clone.1) | dynamic-update-slice | bytes 655364 | tf_op jit(solution)/shard_map/dynamic_update_slice | solution.py:89
  984.9 53.3 %dynamic_update_slice.56 = f32[5,2,32,256,16]{3,4,2,0,1:T(8,128)} dynamic-update-slice(f32[5,2,32,256,16]{3,4,2,0,1:T(8,128)} %dynamic_update_slice.55, f32[5,2,32,16,16]{3,4,2,0,1:T(8,128)S(1)} %copy.70, s32[]{:T(128)} %constant.91.clone.1, s32[]{:T(128)} %constant.91.clone.1, s32[]{:T(128)} %constant.91.clone.1, s32[]{:T(128)S(6)} %select_n.111, s32[]{:T(128)} %constant.91.clone.1) | dynamic-update-slice | bytes 655364 | tf_op jit(solution)/shard_map/dynamic_update_slice | solution.py:89
  1040.7 53.3 %dynamic_update_slice.57 = f32[5,2,32,256,16]{3,4,2,0,1:T(8,128)} dynamic-update-slice(f32[5,2,32,256,16]{3,4,2,0,1:T(8,128)} %dynamic_update_slice.56, f32[5,2,32,16,16]{3,4,2,0,1:T(8,128)S(1)} %copy.72, s32[]{:T(128)} %constant.91.clone.1, s32[]{:T(128)} %constant.91.clone.1, s32[]{:T(128)} %constant.91.clone.1, s32[]{:T(128)S(6)} %select_n.112, s32[]{:T(128)} %constant.91.clone.1) | dynamic-update-slice | bytes 655364 | tf_op jit(solution)/shard_map/dynamic_update_slice | solution.py:89
  1096.5 53.3 %dynamic_update_slice.58 = f32[5,2,32,256,16]{3,4,2,0,1:T(8,128)} dynamic-update-slice(f32[5,2,32,256,16]{3,4,2,0,1:T(8,128)} %dynamic_update_slice.57, f32[5,2,32,16,16]{3,4,2,0,1:T(8,128)S(1)} %copy.74, s32[]{:T(128)} %constant.91.clone.1, s32[]{:T(128)} %constant.91.clone.1, s32[]{:T(128)} %constant.91.clone.1, s32[]{:T(128)S(6)} %select_n.113, s32[]{:T(128)} %constant.91.clone.1) | dynamic-update-slice | bytes 655364 | tf_op jit(solution)/shard_map/dynamic_update_slice | solution.py:89
  1152.3 53.3 %dynamic_update_slice.59 = f32[5,2,32,256,16]{3,4,2,0,1:T(8,128)} dynamic-update-slice(f32[5,2,32,256,16]{3,4,2,0,1:T(8,128)} %dynamic_update_slice.58, f32[5,2,32,16,16]{3,4,2,0,1:T(8,128)S(1)} %copy.76, s32[]{:T(128)} %constant.91.clone.1, s32[]{:T(128)} %constant.91.clone.1, s32[]{:T(128)} %constant.91.clone.1, s32[]{:T(128)S(6)} %select_n.114, s32[]{:T(128)} %constant.91.clone.1) | dynamic-update-slice | bytes 655364 | tf_op jit(solution)/shard_map/dynamic_update_slice | solution.py:89
  1208.1 53.3 %dynamic_update_slice.60 = f32[5,2,32,256,16]{3,4,2,0,1:T(8,128)} dynamic-update-slice(f32[5,2,32,256,16]{3,4,2,0,1:T(8,128)} %dynamic_update_slice.59, f32[5,2,32,16,16]{3,4,2,0,1:T(8,128)S(1)} %copy.78, s32[]{:T(128)} %constant.91.clone.1, s32[]{:T(128)} %constant.91.clone.1, s32[]{:T(128)} %constant.91.clone.1, s32[]{:T(128)S(6)} %select_n.115, s32[]{:T(128)} %constant.91.clone.1) | dynamic-update-slice | bytes 655364 | tf_op jit(solution)/shard_map/dynamic_update_slice | solution.py:89
  1263.9 53.3 %dynamic_update_slice.61 = f32[5,2,32,256,16]{3,4,2,0,1:T(8,128)} dynamic-update-slice(f32[5,2,32,256,16]{3,4,2,0,1:T(8,128)} %dynamic_update_slice.60, f32[5,2,32,16,16]{3,4,2,0,1:T(8,128)S(1)} %copy.80, s32[]{:T(128)} %constant.91.clone.1, s32[]{:T(128)} %constant.91.clone.1, s32[]{:T(128)} %constant.91.clone.1, s32[]{:T(128)S(6)} %select_n.116, s32[]{:T(128)} %constant.91.clone.1) | dynamic-update-slice | bytes 655364 | tf_op jit(solution)/shard_map/dynamic_update_slice | solution.py:89
  1319.7 52.7 %dynamic_update_slice.62 = f32[5,2,32,256,16]{3,4,2,0,1:T(8,128)} dynamic-update-slice(f32[5,2,32,256,16]{3,4,2,0,1:T(8,128)} %dynamic_update_slice.61, f32[5,2,32,16,16]{3,4,2,0,1:T(8,128)S(1)} %copy.82, s32[]{:T(128)} %constant.91.clone.1, s32[]{:T(128)} %constant.91.clone.1, s32[]{:T(128)} %constant.91.clone.1, s32[]{:T(128)S(6)} %select_n.117, s32[]{:T(128)} %constant.91.clone.1) | dynamic-update-slice | bytes 655364 | tf_op jit(solution)/shard_map/dynamic_update_slice | solution.py:89
  1391.1 52.7 %dynamic_update_slice.64 = f32[5,2,32,256,16]{3,4,2,0,1:T(8,128)} dynamic-update-slice(f32[5,2,32,256,16]{3,4,2,0,1:T(8,128)} %dynamic_update_slice.63, f32[5,2,32,16,16]{3,4,2,0,1:T(8,128)S(1)} %copy.86, s32[]{:T(128)} %constant.91.clone.1, s32[]{:T(128)} %constant.91.clone.1, s32[]{:T(128)} %constant.91.clone.1, s32[]{:T(128)S(6)} %select_n.119, s32[]{:T(128)} %constant.91.clone.1) | dynamic-update-slice | bytes 655364 | tf_op jit(solution)/shard_map/dynamic_update_slice | solution.py:89
  1446.3 52.7 %dynamic_update_slice.65 = f32[5,2,32,256,16]{3,4,2,0,1:T(8,128)} dynamic-update-slice(f32[5,2,32,256,16]{3,4,2,0,1:T(8,128)} %dynamic_update_slice.64, f32[5,2,32,16,16]{3,4,2,0,1:T(8,128)S(1)} %copy.88, s32[]{:T(128)} %constant.91.clone.1, s32[]{:T(128)} %constant.91.clone.1, s32[]{:T(128)} %constant.91.clone.1, s32[]{:T(128)S(6)} %select_n.120, s32[]{:T(128)} %constant.91.clone.1) | dynamic-update-slice | bytes 655364 | tf_op jit(solution)/shard_map/dynamic_update_slice | solution.py:89
  1501.5 52.7 %dynamic_update_slice.66 = f32[5,2,32,256,16]{3,4,2,0,1:T(8,128)} dynamic-update-slice(f32[5,2,32,256,16]{3,4,2,0,1:T(8,128)} %dynamic_update_slice.65, f32[5,2,32,16,16]{3,4,2,0,1:T(8,128)S(1)} %copy.90, s32[]{:T(128)} %constant.91.clone.1, s32[]{:T(128)} %constant.91.clone.1, s32[]{:T(128)} %constant.91.clone.1, s32[]{:T(128)S(6)} %select_n.121, s32[]{:T(128)} %constant.91.clone.1) | dynamic-update-slice | bytes 655364 | tf_op jit(solution)/shard_map/dynamic_update_slice | solution.py:89
  1556.6 52.7 %dynamic_update_slice.67 = f32[5,2,32,256,16]{3,4,2,0,1:T(8,128)} dynamic-update-slice(f32[5,2,32,256,16]{3,4,2,0,1:T(8,128)} %dynamic_update_slice.66, f32[5,2,32,16,16]{3,4,2,0,1:T(8,128)S(1)} %copy.92, s32[]{:T(128)} %constant.91.clone.1, s32[]{:T(128)} %constant.91.clone.1, s32[]{:T(128)} %constant.91.clone.1, s32[]{:T(128)S(6)} %select_n.122, s32[]{:T(128)} %constant.91.clone.1) | dynamic-update-slice | bytes 655364 | tf_op jit(solution)/shard_map/dynamic_update_slice | solution.py:89
  1611.8 52.7 %dynamic_update_slice.68 = f32[5,2,32,256,16]{3,4,2,0,1:T(8,128)} dynamic-update-slice(f32[5,2,32,256,16]{3,4,2,0,1:T(8,128)} %dynamic_update_slice.67, f32[5,2,32,16,16]{3,4,2,0,1:T(8,128)S(1)} %copy.94, s32[]{:T(128)} %constant.91.clone.1, s32[]{:T(128)} %constant.91.clone.1, s32[]{:T(128)} %constant.91.clone.1, s32[]{:T(128)S(6)} %select_n.123, s32[]{:T(128)} %constant.91.clone.1) | dynamic-update-slice | bytes 655364 | tf_op jit(solution)/shard_map/dynamic_update_slice | solution.py:89
  1666.9 52.8 %dynamic_update_slice.69 = f32[5,2,32,256,16]{3,4,2,0,1:T(8,128)} dynamic-update-slice(f32[5,2,32,256,16]{3,4,2,0,1:T(8,128)} %dynamic_update_slice.68, f32[5,2,32,16,16]{3,4,2,0,1:T(8,128)S(1)} %copy.96, s32[]{:T(128)} %constant.91.clone.1, s32[]{:T(128)} %constant.91.clone.1, s32[]{:T(128)} %constant.91.clone.1, s32[]{:T(128)S(6)} %select_n.124, s32[]{:T(128)} %constant.91.clone.1) | dynamic-update-slice | bytes 655364 | tf_op jit(solution)/shard_map/dynamic_update_slice | solution.py:89
  (145 shorter events, 531.6 us)
Async XLA Ops:
  0.0 496.0 %copy-start = (f32[5,16]{1,0:T(8,128)S(1)}, f32[5,16]{1,0:T(8,128)}, u32[]{:S(2)}) copy-start(f32[5,16]{1,0:T(8,128)} %param.15) | copy-start | bytes 964
  8.8 11.4 copy-start.9
  13.5 16.3 collective-permute-start
  18.2 12.6 collective-permute-start.1
  31.9 13.5 copy-start.6
  477.6 11.4 copy-start.2
  477.6 11.4 copy-start.8
  547.2 30.2 %collective-permute-start.2 = (f32[5,2,32,16,16]{2,4,3,1,0:T(8,128)}, f32[5,2,32,16,16]{2,4,3,1,0:T(8,128)S(1)}, u32[]{:S(2)}, u32[]{:S(2)}) collective-permute-start(f32[5,2,32,16,16]{2,4,3,1,0:T(8,128)} %copy.67), channel_id=1, source_target_pairs={{0,1},{1,0},{2,3},{3,2},{4,5},{5,4},{6,7},{7,6},{8,9},{9,8},{10,11... | collective-permute-start | bytes 983048 | tf_op jit(solution)/shard_map/ppermute | solution.py:88
  550.9 32.1 %collective-permute-start.3 = (f32[5,2,32,16,16]{2,4,3,1,0:T(8,128)}, f32[5,2,32,16,16]{2,4,3,1,0:T(8,128)S(1)}, u32[]{:S(2)}, u32[]{:S(2)}) collective-permute-start(f32[5,2,32,16,16]{2,4,3,1,0:T(8,128)} %copy.69), channel_id=1, source_target_pairs={{0,2},{1,3},{2,0},{3,1},{4,6},{5,7},{6,4},{7,5},{8,10},{9,11},{10,... | collective-permute-start | bytes 983048 | tf_op jit(solution)/shard_map/ppermute | solution.py:88
  557.1 54.1 %collective-permute-start.4 = (f32[5,2,32,16,16]{2,4,3,1,0:T(8,128)}, f32[5,2,32,16,16]{2,4,3,1,0:T(8,128)}, u32[]{:S(2)}, u32[]{:S(2)}) collective-permute-start(f32[5,2,32,16,16]{2,4,3,1,0:T(8,128)} %copy.71), channel_id=1, source_target_pairs={{0,3},{1,2},{2,1},{3,0},{4,7},{5,6},{6,5},{7,4},{8,11},{9,10},{10,... | collective-permute-start | bytes 983048 | tf_op jit(solution)/shard_map/ppermute | solution.py:88
  560.8 52.7 %collective-permute-start.5 = (f32[5,2,32,16,16]{2,4,3,1,0:T(8,128)}, f32[5,2,32,16,16]{2,4,3,1,0:T(8,128)}, u32[]{:S(2)}, u32[]{:S(2)}) collective-permute-start(f32[5,2,32,16,16]{2,4,3,1,0:T(8,128)} %copy.73), channel_id=1, source_target_pairs={{0,4},{1,5},{2,6},{3,7},{4,0},{5,1},{6,2},{7,3},{8,12},{9,13},{10,... | collective-permute-start | bytes 983048 | tf_op jit(solution)/shard_map/ppermute | solution.py:88
  565.8 110.9 %collective-permute-start.6 = (f32[5,2,32,16,16]{2,4,3,1,0:T(8,128)}, f32[5,2,32,16,16]{2,4,3,1,0:T(8,128)}, u32[]{:S(2)}, u32[]{:S(2)}) collective-permute-start(f32[5,2,32,16,16]{2,4,3,1,0:T(8,128)} %copy.75), channel_id=1, source_target_pairs={{0,5},{1,4},{2,7},{3,6},{4,1},{5,0},{6,3},{7,2},{8,13},{9,12},{10,... | collective-permute-start | bytes 983048 | tf_op jit(solution)/shard_map/ppermute | solution.py:88
  577.5 40.2 %copy-start.3 = (f32[5,2,32,16,16]{2,4,3,1,0:T(8,128)}, f32[5,2,32,16,16]{2,4,3,1,0:T(8,128)S(1)}, u32[]{:S(2)}) copy-start(f32[5,2,32,16,16]{2,4,3,1,0:T(8,128)S(1)} %collective-permute-done.2) | copy-start | bytes 983044
  577.5 127.6 %collective-permute-start.7 = (f32[5,2,32,16,16]{2,4,3,1,0:T(8,128)}, f32[5,2,32,16,16]{2,4,3,1,0:T(8,128)}, u32[]{:S(2)}, u32[]{:S(2)}) collective-permute-start(f32[5,2,32,16,16]{2,4,3,1,0:T(8,128)} %copy.77), channel_id=1, source_target_pairs={{0,6},{1,7},{2,4},{3,5},{4,2},{5,3},{6,0},{7,1},{8,14},{9,15},{10,... | collective-permute-start | bytes 983048 | tf_op jit(solution)/shard_map/ppermute | solution.py:88
  582.9 34.7 %copy-start.4 = (f32[5,2,32,16,16]{2,4,3,1,0:T(8,128)}, f32[5,2,32,16,16]{2,4,3,1,0:T(8,128)S(1)}, u32[]{:S(2)}) copy-start(f32[5,2,32,16,16]{2,4,3,1,0:T(8,128)S(1)} %collective-permute-done.3) | copy-start | bytes 983044
  582.9 150.8 %collective-permute-start.8 = (f32[5,2,32,16,16]{2,4,3,1,0:T(8,128)}, f32[5,2,32,16,16]{2,4,3,1,0:T(8,128)}, u32[]{:S(2)}, u32[]{:S(2)}) collective-permute-start(f32[5,2,32,16,16]{2,4,3,1,0:T(8,128)} %copy.79), channel_id=1, source_target_pairs={{0,7},{1,6},{2,5},{3,4},{4,3},{5,2},{6,1},{7,0},{8,15},{9,14},{10,... | collective-permute-start | bytes 983048 | tf_op jit(solution)/shard_map/ppermute | solution.py:88
  611.2 128.2 %collective-permute-start.9 = (f32[5,2,32,16,16]{2,4,3,1,0:T(8,128)}, f32[5,2,32,16,16]{2,4,3,1,0:T(8,128)}, u32[]{:S(2)}, u32[]{:S(2)}) collective-permute-start(f32[5,2,32,16,16]{2,4,3,1,0:T(8,128)} %copy.81), channel_id=1, source_target_pairs={{0,8},{1,9},{2,10},{3,11},{4,12},{5,13},{6,14},{7,15},{8,0},{9,1},... | collective-permute-start | bytes 983048 | tf_op jit(solution)/shard_map/ppermute | solution.py:88
  613.5 127.1 %collective-permute-start.10 = (f32[5,2,32,16,16]{2,4,3,1,0:T(8,128)}, f32[5,2,32,16,16]{2,4,3,1,0:T(8,128)}, u32[]{:S(2)}, u32[]{:S(2)}) collective-permute-start(f32[5,2,32,16,16]{2,4,3,1,0:T(8,128)} %copy.83), channel_id=1, source_target_pairs={{0,9},{1,8},{2,11},{3,10},{4,13},{5,12},{6,15},{7,14},{8,1},{9,0},... | collective-permute-start | bytes 983048 | tf_op jit(solution)/shard_map/ppermute | solution.py:88
  676.7 227.4 %collective-permute-start.11 = (f32[5,2,32,16,16]{2,4,3,1,0:T(8,128)}, f32[5,2,32,16,16]{2,4,3,1,0:T(8,128)S(1)}, u32[]{:S(2)}, u32[]{:S(2)}) collective-permute-start(f32[5,2,32,16,16]{2,4,3,1,0:T(8,128)} %copy.85), channel_id=1, source_target_pairs={{0,10},{1,11},{2,8},{3,9},{4,14},{5,15},{6,12},{7,13},{8,2},{9,3},... | collective-permute-start | bytes 983048 | tf_op jit(solution)/shard_map/ppermute | solution.py:88
  705.0 738.8 %collective-permute-start.12 = (f32[5,2,32,16,16]{2,4,3,1,0:T(8,128)}, f32[5,2,32,16,16]{2,4,3,1,0:T(8,128)}, u32[]{:S(2)}, u32[]{:S(2)}) collective-permute-start(f32[5,2,32,16,16]{2,4,3,1,0:T(8,128)} %copy.87), channel_id=1, source_target_pairs={{0,11},{1,10},{2,9},{3,8},{4,15},{5,14},{6,13},{7,12},{8,3},{9,2},... | collective-permute-start | bytes 983048 | tf_op jit(solution)/shard_map/ppermute | solution.py:88
  733.7 765.3 %collective-permute-start.13 = (f32[5,2,32,16,16]{2,4,3,1,0:T(8,128)}, f32[5,2,32,16,16]{2,4,3,1,0:T(8,128)}, u32[]{:S(2)}, u32[]{:S(2)}) collective-permute-start(f32[5,2,32,16,16]{2,4,3,1,0:T(8,128)} %copy.89), channel_id=1, source_target_pairs={{0,12},{1,13},{2,14},{3,15},{4,8},{5,9},{6,10},{7,11},{8,4},{9,5},... | collective-permute-start | bytes 983048 | tf_op jit(solution)/shard_map/ppermute | solution.py:88
  739.4 814.8 %collective-permute-start.14 = (f32[5,2,32,16,16]{2,4,3,1,0:T(8,128)}, f32[5,2,32,16,16]{2,4,3,1,0:T(8,128)}, u32[]{:S(2)}, u32[]{:S(2)}) collective-permute-start(f32[5,2,32,16,16]{2,4,3,1,0:T(8,128)} %copy.91), channel_id=1, source_target_pairs={{0,13},{1,12},{2,15},{3,14},{4,9},{5,8},{6,11},{7,10},{8,5},{9,4},... | collective-permute-start | bytes 983048 | tf_op jit(solution)/shard_map/ppermute | solution.py:88
  740.6 868.7 %collective-permute-start.15 = (f32[5,2,32,16,16]{2,4,3,1,0:T(8,128)}, f32[5,2,32,16,16]{2,4,3,1,0:T(8,128)}, u32[]{:S(2)}, u32[]{:S(2)}) collective-permute-start(f32[5,2,32,16,16]{2,4,3,1,0:T(8,128)} %copy.93), channel_id=1, source_target_pairs={{0,14},{1,15},{2,12},{3,13},{4,10},{5,11},{6,8},{7,9},{8,6},{9,7},... | collective-permute-start | bytes 983048 | tf_op jit(solution)/shard_map/ppermute | solution.py:88
  904.1 760.3 %collective-permute-start.16 = (f32[5,2,32,16,16]{2,4,3,1,0:T(8,128)}, f32[5,2,32,16,16]{2,4,3,1,0:T(8,128)}, u32[]{:S(2)}, u32[]{:S(2)}) collective-permute-start(f32[5,2,32,16,16]{2,4,3,1,0:T(8,128)} %copy.95), channel_id=1, source_target_pairs={{0,15},{1,14},{2,13},{3,12},{4,11},{5,10},{6,9},{7,8},{8,7},{9,6},... | collective-permute-start | bytes 983048 | tf_op jit(solution)/shard_map/ppermute | solution.py:88
  (3 other events, 13.6 us)
